TPU v7x, 32 devices: a whole 2x2x4 slice. The times are simulated.
32 devices in a mesh: row: 4 (over x, core), col: 8 (over z, y).
Axes of the slice: x: 2, y: 2, z: 4, core: 2. Of those that a mesh axis runs over, the one named last changes fastest.
Arguments:
- points: float32 [16, 8192], P(None, ('row', 'col')), may hold values from -6 to 6
- lengthscale: float32 [16], replicated, may hold values from 2 to 8
- signal: float32 [1], replicated, may hold values from 0.5 to 2
- noise: float32 [1], replicated, may hold values from 0.05 to 0.5
- targets: float32 [8192], P(('row', 'col')), may hold values from -12 to 12
- probe_bits: int32 [31, 8192], P(None, ('row', 'col')), may hold values from 0 to 1
Outputs:
- solution: float32 [32, 8192], P(None, ('row', 'col'))
- residual: float32 [32, 8192], P(None, ('row', 'col'))
All inputs are finite; a program needn't handle non-finite values.
Results may differ from a plain program's by a relative error of at most 0.0013.
Values sent between devices are 32-bit elements; how exact they have to be, the bound alone decides.
No kernel may reach another device: no remote copies, remote signals or barrier semaphores. Data moves between devices by JAX's collectives and lax.ppermute only.
A program may use at most 128 MiB of HBM per device.

v0:
```python
import jax
import jax.numpy as jnp
from jax import lax
from jax.sharding import PartitionSpec as P

ITERS = 3
ROOT_FIVE = 5.0**0.5


def matern_tile(row_scaled, col_scaled, signal_value):
    row_sq = jnp.sum(row_scaled * row_scaled, axis=0)
    col_sq = jnp.sum(col_scaled * col_scaled, axis=0)
    cross_term = lax.dot_general(
        row_scaled,
        col_scaled,
        (((0,), (0,)), ((), ())),
        precision=lax.Precision.HIGHEST,
        preferred_element_type=jnp.float32,
    )
    dist_sq = jnp.maximum(row_sq[:, None] + col_sq[None, :] - 2.0 * cross_term, 0.0)
    radius = jnp.sqrt(dist_sq)
    return (
        signal_value
        * (1.0 + ROOT_FIVE * radius + 5.0 / 3.0 * dist_sq)
        * jnp.exp(-ROOT_FIVE * radius)
    )


def row_blocks(row_scaled):
    row_total = row_scaled.shape[1]
    block_rows = min(1024, row_total)
    block_count = row_total // block_rows
    return row_scaled.reshape(row_scaled.shape[0], block_count, block_rows).transpose(1, 0, 2)


def apply_tile(row_scaled, col_scaled, signal_value, vectors):
    row_total = row_scaled.shape[1]
    stacked = row_blocks(row_scaled)

    def one_block(row_block):
        kernel_tile = matern_tile(row_block, col_scaled, signal_value)
        return lax.dot_general(
            vectors,
            kernel_tile,
            (((1,), (1,)), ((), ())),
            precision=lax.Precision.HIGHEST,
            preferred_element_type=jnp.float32,
        )

    pieces = lax.map(one_block, stacked)
    return pieces.transpose(1, 0, 2).reshape(vectors.shape[0], row_total)


def squares(residual):
    return lax.psum(jnp.sum(residual * residual, axis=1), ("row", "col"))


def body(points, lengthscale, signal, noise, targets, probe_bits):
    scaled = points / lengthscale[:, None]
    signs = 2.0 * probe_bits.astype(jnp.float32) - 1.0
    right_side = jnp.concatenate([targets[None, :], signs], axis=0)
    signal_value = signal[0]
    noise_value = noise[0]
    every_point = lax.all_gather(scaled, ("row", "col"), axis=1, tiled=True)
    solution = jnp.zeros_like(right_side)
    residual = right_side
    direction = right_side
    norm_now = squares(residual)
    for step in range(ITERS):
        summed = apply_tile(
            scaled,
            every_point,
            signal_value,
            lax.all_gather(direction, ("row", "col"), axis=1, tiled=True),
        )
        image = summed + noise_value * direction
        curved = lax.psum(jnp.sum(direction * image, axis=1), ("row", "col"))
        alpha = norm_now / curved
        solution = solution + alpha[:, None] * direction
        residual = residual - alpha[:, None] * image
        if step + 1 < ITERS:
            norm_next = squares(residual)
            direction = residual + (norm_next / norm_now)[:, None] * direction
            norm_now = norm_next
    return (solution, residual)


def solution(mesh):
    return jax.shard_map(
        body,
        mesh=mesh,
        in_specs=(
            P(None, ("row", "col")),
            P(),
            P(),
            P(),
            P(("row", "col")),
            P(None, ("row", "col")),
        ),
        out_specs=(P(None, ("row", "col")), P(None, ("row", "col"))),
        check_vma=False,
    )
```

profile of v0, /device:TPU:0, one launch (start us, length us, event | category | flops | bytes accessed | tf_op | source)
XLA Modules:
  0.0 442.8 jit_solution(3945853298160864915)
XLA Ops:
  7.2 0.0 all-gather.4.cloned.1.call-start
  7.2 0.8 multiply_add_fusion.3
  8.0 1.3 pad_maximum_fusion
  9.3 0.0 all-gather.4.cloned.1.call-update
  9.3 0.0 all-gather.6.cloned.1.call-start
  10.6 0.8 multiply_reduce_fusion.7
  11.5 73.2 %all_gather.13 = f32[16,8192]{1,0:T(8,128)S(1)} all-gather(f32[16,256]{1,0:T(8,128)S(1)} %get-tuple-element.51), channel_id=1, replica_groups=mesh['row'=4,'col'=8] {'row','col'}, dimensions={1}, use_global_device_ids=true | all-gather | bytes 540672 | tf_op jit(solution)/shard_map/all_gather | solution.py:64
  84.6 0.1 multiply_reduce_fusion
  84.7 0.0 copy-start.2
  84.7 14.0 %exponential_multiply_fusion = f32[256,8192]{1,0:T(8,128)} fusion(f32[16,256]{1,0:T(8,128)S(1)} %get-tuple-element.51, f32[16,8192]{1,0:T(8,128)S(1)} %all_gather.13, f32[8192]{0:T(1024)S(1)} %multiply_reduce_fusion, f32[256]{0:T(256)S(1)} %get-tuple-element.50, f32[]{:T(128)} %bitcast.11), kind=kOutput, calls=%fused_computation.3 | convolution fusion | flops 425721856 | bytes 8963076 | tf_op jit(solution)/shard_map/while/body/eval_jaxpr/dot_general | solution.py:13
  98.7 0.0 copy-start.3
  98.7 0.0 all-gather.4.cloned.1.call-done
  98.7 0.0 copy-done.2
  98.8 11.2 %multiply_reduce_fusion.5 = (f32[32]{0:T(128)S(1)}, f32[32]{0:T(128)S(1)}, f32[32,256]{1,0:T(8,128)S(1)}) fusion(f32[32,256]{1,0:T(8,128)S(1)} %copy-done.2, f32[]{:T(128)} %bitcast.12, f32[32,8192]{1,0:T(8,128)} %all-gather.4.cloned.1.call-done, f32[256,8192]{1,0:T(8,128)} %exponential_multiply_fusion), kind=kOutput, calls=%fused_computation.19 | convolution fusion | flops 805355456 | bytes 9502980 | tf_op jit(solution)/shard_map/while/body/eval_jaxpr/dot_general | solution.py:42
  109.9 37.1 %all-reduce = (f32[32]{0:T(128)S(1)}, f32[32]{0:T(128)S(1)}) all-reduce(f32[32]{0:T(128)S(1)} %get-tuple-element.39, f32[32]{0:T(128)S(1)} %get-tuple-element.38), channel_id=1, replica_groups=mesh['row'=4,'col'=8] {'row','col'}, use_global_device_ids=true, to_apply=%region_1.0 | all-reduce | flops 64 | bytes 512 | tf_op jit(solution)/shard_map/psum | solution.py:55
  147.0 0.0 copy-done.3
  147.0 0.2 multiply_reduce_fusion.4
  147.2 41.5 %psum.44 = f32[32]{0:T(128)S(1)} all-reduce(f32[32]{0:T(128)S(1)} %multiply_reduce_fusion.4), channel_id=1, replica_groups=mesh['row'=4,'col'=8] {'row','col'}, use_global_device_ids=true, to_apply=%region_7.8 | all-reduce | flops 32 | bytes 256 | tf_op jit(solution)/shard_map/psum | solution.py:55
  188.7 0.7 multiply_add_fusion.2
  189.4 0.0 copy-start
  189.4 0.0 all-gather.6.cloned.1.call-update
  189.5 0.0 all-gather.8.cloned.1.call-start
  189.5 51.3 %all-gather.6.cloned.1.call-done = f32[32,8192]{1,0:T(8,128)} async-done(((f32[32,256]{1,0:T(8,128)}), f32[32,8192]{1,0:T(8,128)}) %all-gather.6.cloned.1.call-update) | async-done | bytes 1048592 | tf_op jit(solution)/shard_map/all_gather | solution.py:74
  240.8 11.1 %multiply_reduce_fusion.3 = (f32[32]{0:T(128)S(1)}, f32[32,256]{1,0:T(8,128)S(1)}) fusion(f32[32,256]{1,0:T(8,128)} %multiply_add_fusion.2, f32[]{:T(128)} %bitcast.14, f32[32,8192]{1,0:T(8,128)} %all-gather.6.cloned.1.call-done, f32[256,8192]{1,0:T(8,128)} %exponential_multiply_fusion), kind=kOutput, calls=%fused_computation.15 | convolution fusion | flops 805339136 | bytes 9502852 | tf_op jit(solution)/shard_map/while/body/eval_jaxpr/dot_general | solution.py:42
  251.9 40.3 %psum.45 = f32[32]{0:T(128)S(1)} all-reduce(f32[32]{0:T(128)S(1)} %get-tuple-element.61), channel_id=1, replica_groups=mesh['row'=4,'col'=8] {'row','col'}, use_global_device_ids=true, to_apply=%region_9.10 | all-reduce | flops 32 | bytes 256 | tf_op jit(solution)/shard_map/psum | solution.py:77
  292.1 0.2 multiply_reduce_fusion.2
  292.3 39.2 %psum.46 = f32[32]{0:T(128)S(1)} all-reduce(f32[32]{0:T(128)S(1)} %get-tuple-element.48), channel_id=1, replica_groups=mesh['row'=4,'col'=8] {'row','col'}, use_global_device_ids=true, to_apply=%region_11.12 | all-reduce | flops 32 | bytes 256 | tf_op jit(solution)/shard_map/psum | solution.py:55
  331.5 0.0 copy-done
  331.5 0.7 multiply_add_fusion.1
  332.2 0.0 copy-start.1
  332.2 0.0 all-gather.8.cloned.1.call-update
  332.3 52.0 %all-gather.8.cloned.1.call-done = f32[32,8192]{1,0:T(8,128)} async-done(((f32[32,256]{1,0:T(8,128)}), f32[32,8192]{1,0:T(8,128)}) %all-gather.8.cloned.1.call-update) | async-done | bytes 1048592 | tf_op jit(solution)/shard_map/all_gather | solution.py:74
  384.2 11.1 %multiply_reduce_fusion.1 = (f32[32]{0:T(128)S(1)}, f32[32,256]{1,0:T(8,128)S(1)}) fusion(f32[32,256]{1,0:T(8,128)} %multiply_add_fusion.1, f32[]{:T(128)} %bitcast.13, f32[32,8192]{1,0:T(8,128)} %all-gather.8.cloned.1.call-done, f32[256,8192]{1,0:T(8,128)} %exponential_multiply_fusion), kind=kOutput, calls=%fused_computation.11 | convolution fusion | flops 805339136 | bytes 9502852 | tf_op jit(solution)/shard_map/while/body/eval_jaxpr/dot_general | solution.py:42
  395.3 40.3 %psum.47 = f32[32]{0:T(128)S(1)} all-reduce(f32[32]{0:T(128)S(1)} %get-tuple-element.63), channel_id=1, replica_groups=mesh['row'=4,'col'=8] {'row','col'}, use_global_device_ids=true, to_apply=%region_13.14 | all-reduce | flops 32 | bytes 256 | tf_op jit(solution)/shard_map/psum | solution.py:77
  435.5 0.0 copy-done.1
  435.5 0.7 multiply_subtract_fusion
  (5 shorter events, 0.0 us)
Async XLA Ops:
  7.2 91.6 %all-gather.4.cloned.1.call-start = ((), (), s32[]{:S(2)}) async-start(), calls=%async_computation | async-start | bytes 1081344 | tf_op jit(solution)/shard_map/all_gather | solution.py:74
  9.3 231.5 %all-gather.6.cloned.1.call-start = ((), (), s32[]{:S(2)}) async-start(), calls=%async_computation.1 | async-start | bytes 1081344 | tf_op jit(solution)/shard_map/all_gather | solution.py:74
  84.7 14.0 %copy-start.2 = (f32[32,256]{1,0:T(8,128)S(1)}, f32[32,256]{1,0:T(8,128)}, u32[]{:S(2)}) copy-start(f32[32,256]{1,0:T(8,128)} %pad_maximum_fusion) | copy-start | bytes 98308
  98.7 48.3 %copy-start.3 = (f32[256]{0:T(256)S(1)}, f32[256]{0:T(256)}, u32[]{:S(2)}) copy-start(f32[256]{0:T(256)} %param.10) | copy-start | bytes 3076
  189.4 142.1 %copy-start = (f32[32,256]{1,0:T(8,128)S(1)}, f32[32,256]{1,0:T(8,128)}, u32[]{:S(2)}) copy-start(f32[32,256]{1,0:T(8,128)} %multiply_add_fusion.2) | copy-start | bytes 98308
  189.5 194.7 %all-gather.8.cloned.1.call-start = ((), (), s32[]{:S(2)}) async-start(), calls=%async_computation.2 | async-start | bytes 1081344 | tf_op jit(solution)/shard_map/all_gather | solution.py:74
  332.2 103.3 %copy-start.1 = (f32[32,256]{1,0:T(8,128)S(1)}, f32[32,256]{1,0:T(8,128)}, u32[]{:S(2)}) copy-start(f32[32,256]{1,0:T(8,128)} %multiply_add_fusion.1) | copy-start | bytes 98308
Sparse Core Ops, SparseCore 0:
  11.4 54.6 all-gather.3
  189.6 51.1 all-gather.5
  332.4 51.7 all-gather.7
where the time goes:
time: 444 us; the launch traced here: 443 us
  blocking collectives  272 us (61%)
  waiting for transfers between devices  103 us (23%)
  matrix products  47.3 us (11%)
  between operations  15.1 us (3%)
  other arithmetic  5.46 us (1%)
    psum x3, blocking collectives, squares(): return lax.psum(jnp.sum(residual * residual, axis=1), ('row', 'col'))  118 us
    all_gather x3, waiting for transfers between devices, body(): lax.all_gather(direction, ('row', 'col'), axis=1, tiled=True)  103 us
    psum x2, blocking collectives, body(): curved = lax.psum(jnp.sum(direction * image, axis=1), ('row', 'col'))  80.5 us
    all_gather x1, blocking collectives, body(): every_point = lax.all_gather(scaled, ('row', 'col'), axis=1, tiled=True)  73.2 us
    dot_general x3, matrix products, one_block(): lax.dot_general(vectors, kernel_tile, (((1,), (1,)), ((), ())), precision...  33.3 us
    dot_general x1, matrix products, matern_tile(): lax.dot_general(row_scaled, col_scaled, (((0,), (0,)), ((), ())), precisi...  14 us
  transfers between devices with their start and end apart: 3, of which 2 were waited for; matrix products, arithmetic and copies ran while one was open for 3% of the time, Pallas kernels for 0%

commit v1 on v0

--- a/solution.py
+++ b/solution.py
@@ -1,10 +1,19 @@
+import functools
 import jax
 import jax.numpy as jnp
 from jax import lax
 from jax.sharding import PartitionSpec as P
+from jax.lax import all_gather
 
 ITERS = 3
 ROOT_FIVE = 5.0**0.5
+
+
+def terms_map(local_values, which_axis):
+    return jnp.concatenate(all_gather(local_values, axis_name=which_axis), 1)
+
+
+advance_edges = functools.partial(terms_map, which_axis=("row", "col"))
 
 
 def matern_tile(row_scaled, col_scaled, signal_value):
@@ -67,12 +76,7 @@
     direction = right_side
     norm_now = squares(residual)
     for step in range(ITERS):
-        summed = apply_tile(
-            scaled,
-            every_point,
-            signal_value,
-            lax.all_gather(direction, ("row", "col"), axis=1, tiled=True),
-        )
+        summed = apply_tile(scaled, every_point, signal_value, advance_edges(direction))
         image = summed + noise_value * direction
         curved = lax.psum(jnp.sum(direction * image, axis=1), ("row", "col"))
         alpha = norm_now / curved

time: 444 us -> 446 us (level)
  no operation moved by 1% of the time
where the time goes in v1:
time: 446 us; the launch traced here: 445 us
  blocking collectives  270 us (61%)
  waiting for transfers between devices  107 us (24%)
  matrix products  43.5 us (10%)
  between operations  15.1 us (3%)
  other arithmetic  5.46 us (1%)
    psum x3, blocking collectives, squares(): return lax.psum(jnp.sum(residual * residual, axis=1), ('row', 'col'))  119 us
    all_gather x3, waiting for transfers between devices, terms_map(): return jnp.concatenate(all_gather(local_values, axis_name=which_axis), 1)  107 us
    psum x2, blocking collectives, body(): curved = lax.psum(jnp.sum(direction * image, axis=1), ('row', 'col'))  78.6 us
    all_gather x1, blocking collectives, body(): every_point = lax.all_gather(scaled, ('row', 'col'), axis=1, tiled=True)  73 us
    dot_general x3, matrix products, one_block(): lax.dot_general(vectors, kernel_tile, (((1,), (1,)), ((), ())), precision...  29.5 us
    dot_general x1, matrix products, matern_tile(): lax.dot_general(row_scaled, col_scaled, (((0,), (0,)), ((), ())), precisi...  14 us
  transfers between devices with their start and end apart: 3, of which 2 were waited for; matrix products, arithmetic and copies ran while one was open for 3% of the time, Pallas kernels for 0%

profile of v1, /device:TPU:0, one launch (start us, length us, event | category | flops | bytes accessed | tf_op | source)
XLA Modules:
  0.0 445.3 jit_solution(10830313072789879165)
XLA Ops:
  7.2 0.0 all-gather.7.cloned.1.call-start
  7.2 0.8 multiply_add_fusion.3
  8.0 1.3 pad_maximum_fusion
  9.3 0.0 all-gather.7.cloned.1.call-update
  9.3 0.0 all-gather.9.cloned.1.call-start
  10.6 0.8 multiply_reduce_fusion.7
  11.5 73.0 %all_gather.19 = f32[16,8192]{1,0:T(8,128)S(1)} all-gather(f32[16,256]{1,0:T(8,128)S(1)} %get-tuple-element.51), channel_id=1, replica_groups=mesh['row'=4,'col'=8] {'row','col'}, dimensions={1}, use_global_device_ids=true | all-gather | bytes 540672 | tf_op jit(solution)/shard_map/all_gather | solution.py:73
  84.4 0.1 multiply_reduce_fusion
  84.5 0.0 copy-start.2
  84.5 14.0 %exponential_multiply_fusion = f32[256,8192]{1,0:T(8,128)} fusion(f32[16,256]{1,0:T(8,128)S(1)} %get-tuple-element.51, f32[16,8192]{1,0:T(8,128)S(1)} %all_gather.19, f32[8192]{0:T(1024)S(1)} %multiply_reduce_fusion, f32[256]{0:T(256)S(1)} %get-tuple-element.50, f32[]{:T(128)} %bitcast.29), kind=kOutput, calls=%fused_computation.3 | convolution fusion | flops 425721856 | bytes 8963076 | tf_op jit(solution)/shard_map/while/body/eval_jaxpr/dot_general | solution.py:22
  98.5 0.0 copy-start.3
  98.5 0.0 all-gather.7.cloned.1.call-done
  98.5 1.3 copy.11
  99.8 0.0 copy-done.2
  99.9 9.8 %multiply_reduce_fusion.5 = (f32[32]{0:T(128)S(1)}, f32[32]{0:T(128)S(1)}, f32[32,256]{1,0:T(8,128)S(1)}) fusion(f32[32,256]{1,0:T(8,128)S(1)} %copy-done.2, f32[]{:T(128)} %bitcast.30, f32[32,8192]{1,0:T(8,128)S(1)} %bitcast.33, f32[256,8192]{1,0:T(8,128)} %exponential_multiply_fusion), kind=kOutput, calls=%fused_computation.19 | convolution fusion | flops 805355456 | bytes 9502980 | tf_op jit(solution)/shard_map/while/body/eval_jaxpr/dot_general | solution.py:51
  109.7 36.9 %all-reduce = (f32[32]{0:T(128)S(1)}, f32[32]{0:T(128)S(1)}) all-reduce(f32[32]{0:T(128)S(1)} %get-tuple-element.39, f32[32]{0:T(128)S(1)} %get-tuple-element.38), channel_id=1, replica_groups=mesh['row'=4,'col'=8] {'row','col'}, use_global_device_ids=true, to_apply=%region_1.0 | all-reduce | flops 64 | bytes 512 | tf_op jit(solution)/shard_map/psum | solution.py:64
  146.6 0.0 copy-done.3
  146.6 0.2 multiply_reduce_fusion.4
  146.7 41.9 %psum.44 = f32[32]{0:T(128)S(1)} all-reduce(f32[32]{0:T(128)S(1)} %multiply_reduce_fusion.4), channel_id=1, replica_groups=mesh['row'=4,'col'=8] {'row','col'}, use_global_device_ids=true, to_apply=%region_7.8 | all-reduce | flops 32 | bytes 256 | tf_op jit(solution)/shard_map/psum | solution.py:64
  188.6 0.7 multiply_add_fusion.2
  189.3 0.0 copy-start
  189.3 0.0 all-gather.9.cloned.1.call-update
  189.3 0.2 all-gather.11.cloned.1.call-start
  189.6 53.1 %all-gather.9.cloned.1.call-done = f32[1024,256]{1,0:T(8,128)} async-done(((f32[32,256]{1,0:T(8,128)}), f32[1024,256]{1,0:T(8,128)}) %all-gather.9.cloned.1.call-update) | async-done | bytes 1048592 | tf_op jit(solution)/shard_map/all_gather | solution.py:13
  242.7 1.3 copy.12
  244.0 9.8 %multiply_reduce_fusion.3 = (f32[32]{0:T(128)S(1)}, f32[32,256]{1,0:T(8,128)S(1)}) fusion(f32[32,256]{1,0:T(8,128)} %multiply_add_fusion.2, f32[]{:T(128)} %bitcast.32, f32[32,8192]{1,0:T(8,128)S(1)} %bitcast.35, f32[256,8192]{1,0:T(8,128)} %exponential_multiply_fusion), kind=kOutput, calls=%fused_computation.15 | convolution fusion | flops 805339136 | bytes 9502852 | tf_op jit(solution)/shard_map/while/body/eval_jaxpr/dot_general | solution.py:51
  253.8 39.3 %psum.45 = f32[32]{0:T(128)S(1)} all-reduce(f32[32]{0:T(128)S(1)} %get-tuple-element.61), channel_id=1, replica_groups=mesh['row'=4,'col'=8] {'row','col'}, use_global_device_ids=true, to_apply=%region_9.10 | all-reduce | flops 32 | bytes 256 | tf_op jit(solution)/shard_map/psum | solution.py:81
  293.2 0.2 multiply_reduce_fusion.2
  293.4 39.8 %psum.46 = f32[32]{0:T(128)S(1)} all-reduce(f32[32]{0:T(128)S(1)} %get-tuple-element.48), channel_id=1, replica_groups=mesh['row'=4,'col'=8] {'row','col'}, use_global_device_ids=true, to_apply=%region_11.12 | all-reduce | flops 32 | bytes 256 | tf_op jit(solution)/shard_map/psum | solution.py:64
  333.2 0.0 copy-done
  333.2 0.7 multiply_add_fusion.1
  333.9 0.0 copy-start.1
  333.9 0.0 all-gather.11.cloned.1.call-update
  333.9 53.6 %all-gather.11.cloned.1.call-done = f32[1024,256]{1,0:T(8,128)} async-done(((f32[32,256]{1,0:T(8,128)}), f32[1024,256]{1,0:T(8,128)}) %all-gather.11.cloned.1.call-update) | async-done | bytes 1048592 | tf_op jit(solution)/shard_map/all_gather | solution.py:13
  387.6 1.3 copy.13
  388.9 9.8 %multiply_reduce_fusion.1 = (f32[32]{0:T(128)S(1)}, f32[32,256]{1,0:T(8,128)S(1)}) fusion(f32[32,256]{1,0:T(8,128)} %multiply_add_fusion.1, f32[]{:T(128)} %bitcast.31, f32[32,8192]{1,0:T(8,128)S(1)} %bitcast.34, f32[256,8192]{1,0:T(8,128)} %exponential_multiply_fusion), kind=kOutput, calls=%fused_computation.11 | convolution fusion | flops 805339136 | bytes 9502852 | tf_op jit(solution)/shard_map/while/body/eval_jaxpr/dot_general | solution.py:51
  398.7 39.3 %psum.47 = f32[32]{0:T(128)S(1)} all-reduce(f32[32]{0:T(128)S(1)} %get-tuple-element.63), channel_id=1, replica_groups=mesh['row'=4,'col'=8] {'row','col'}, use_global_device_ids=true, to_apply=%region_13.14 | all-reduce | flops 32 | bytes 256 | tf_op jit(solution)/shard_map/psum | solution.py:81
  438.0 0.0 copy-done.1
  438.0 0.7 multiply_subtract_fusion
  (5 shorter events, 0.0 us)
Async XLA Ops:
  7.2 91.4 %all-gather.7.cloned.1.call-start = ((), (), s32[]{:S(2)}) async-start(), calls=%async_computation | async-start | bytes 1081344 | tf_op jit(solution)/shard_map/all_gather | solution.py:13
  9.3 233.4 %all-gather.9.cloned.1.call-start = ((), (), s32[]{:S(2)}) async-start(), calls=%async_computation.1 | async-start | bytes 1081344 | tf_op jit(solution)/shard_map/all_gather | solution.py:13
  84.5 15.3 %copy-start.2 = (f32[32,256]{1,0:T(8,128)S(1)}, f32[32,256]{1,0:T(8,128)}, u32[]{:S(2)}) copy-start(f32[32,256]{1,0:T(8,128)} %pad_maximum_fusion) | copy-start | bytes 98308
  98.5 48.0 %copy-start.3 = (f32[256]{0:T(256)S(1)}, f32[256]{0:T(256)}, u32[]{:S(2)}) copy-start(f32[256]{0:T(256)} %param.10) | copy-start | bytes 3076
  189.3 143.9 %copy-start = (f32[32,256]{1,0:T(8,128)S(1)}, f32[32,256]{1,0:T(8,128)}, u32[]{:S(2)}) copy-start(f32[32,256]{1,0:T(8,128)} %multiply_add_fusion.2) | copy-start | bytes 98308
  189.3 198.2 %all-gather.11.cloned.1.call-start = ((), (), s32[]{:S(2)}) async-start(), calls=%async_computation.2 | async-start | bytes 1081344 | tf_op jit(solution)/shard_map/all_gather | solution.py:13
  333.9 104.1 %copy-start.1 = (f32[32,256]{1,0:T(8,128)S(1)}, f32[32,256]{1,0:T(8,128)}, u32[]{:S(2)}) copy-start(f32[32,256]{1,0:T(8,128)} %multiply_add_fusion.1) | copy-start | bytes 98308
Sparse Core Ops, SparseCore 0:
  11.6 56.4 all-gather.6
  189.5 53.1 all-gather.8
  334.0 53.4 all-gather.10
